TPU v7x, 256 devices: a whole 4x4x8 slice. The times are simulated.
256 devices in a mesh: seq: 64 (over x, z, core), head: 4 (over y).
Axes of the slice: x: 4, y: 4, z: 8, core: 2. Of those that a mesh axis runs over, the one named last changes fastest.
Arguments:
- queries: bfloat16 [32768, 4096], P('seq', 'head'), may hold values from -120 to 120
- keys: bfloat16 [32768, 1024], P('seq', 'head'), may hold values from -4 to 4
- values: bfloat16 [32768, 1024], P('seq', 'head'), may hold values from -6 to 6
- doc_start: int32 [32768], P('seq'), may hold values from 0 to 32767, as said below
- hop_counts: int32 [64], P('seq'), may hold values from 0 to 4, as said below
- loss_mask: int32 [32768], P('seq'), may hold values from 0 to 1, as said below
Outputs:
- attention: bfloat16 [32768, 4096], P('seq', 'head')
- objective: float32 [], replicated
Inputs may be any that keep to these rules, and one draw needn't show every extreme that they name: doc_start is nondecreasing; doc_start[doc_start[i]] = doc_start[i] <= i; a document holds at most 2048 tokens, and some document holds exactly that many in every draw. hop_counts[b] = b - floor(doc_start[b * 512] / 512); the most, 4, is reached in every draw. loss_mask[0] = 1.
All inputs are finite; a program needn't handle non-finite values.
Results may differ from a plain program's by a relative error of at most 0.0035.
Values may be sent and summed in bfloat16 or wider, within the bound.
A program may use at most 128 MiB of HBM per device.

v0:
```python
import functools
import math

import jax
import jax.numpy as jnp
from jax import lax
from jax.sharding import Mesh
from jax.sharding import PartitionSpec as P

QUERY_HEADS = 32
KEY_VALUE_HEADS = 8
HEAD_WIDTH = 128
HOPS = 4
SEQ = ("seq_0", "seq_1", "seq_2")
SEQ_HEAD = ("seq_0", "seq_1", "seq_2", "head")


def passed_along(shard, axis, by):
    devices = lax.axis_size(axis)
    pairs = [(i, i + by) for i in range(devices) if 0 <= i + by < devices]
    return lax.ppermute(shard, axis, pairs)


def over_axes(shard, axes):
    return functools.reduce(lax.psum, axes, shard)


def attend_block(
    carry, key_block, value_block, distance, grouped_queries, doc_start, block_index, hop_limit
):
    top_old, total_old, weighted = carry
    rows = grouped_queries.shape[0]
    scores = jnp.einsum(
        "tgqd,sgd->tgqs", grouped_queries, key_block, preferred_element_type=jnp.float32
    ) * (1.0 / math.sqrt(HEAD_WIDTH))
    key_place = (block_index - distance) * rows + jnp.arange(rows, dtype=jnp.int32)
    query_place = block_index * rows + jnp.arange(rows, dtype=jnp.int32)
    seen = (
        (key_place[None, :] >= doc_start[:, None])
        & (key_place[None, :] <= query_place[:, None])
        & (distance <= hop_limit)
    )
    seen = seen[:, None, None, :]
    masked = jnp.where(seen, scores, jnp.float32(-1e30))
    top_new = jnp.maximum(top_old, jnp.max(masked, axis=-1))
    ratio_old = jnp.exp(top_old - top_new)
    weights = jnp.where(seen, jnp.exp(masked - top_new[..., None]), jnp.float32(0.0))
    total_new = total_old * ratio_old + jnp.sum(weights, axis=-1)
    rounded = weights.astype(jnp.bfloat16)
    update = jnp.einsum("tgqs,sgd->tgqd", rounded, value_block, preferred_element_type=jnp.float32)
    return (top_new, total_new, weighted * ratio_old[..., None] + update)


def on_device(queries, keys, values, doc_start, hop_counts, loss_mask):
    rows = queries.shape[0]
    kv_heads = keys.shape[1] // HEAD_WIDTH
    group_size = QUERY_HEADS // KEY_VALUE_HEADS
    block_index = lax.axis_index(SEQ)
    hop_limit = hop_counts[0]
    grouped_queries = queries.reshape(rows, kv_heads, group_size, HEAD_WIDTH)
    carry = (
        jnp.full((rows, kv_heads, group_size), -1e30, jnp.float32),
        jnp.zeros((rows, kv_heads, group_size), jnp.float32),
        jnp.zeros((rows, kv_heads, group_size, HEAD_WIDTH), jnp.float32),
    )

    def absorb(state, key_part, value_part, distance):
        key_block = key_part.reshape(rows, kv_heads, HEAD_WIDTH)
        value_block = value_part.reshape(rows, kv_heads, HEAD_WIDTH)
        return attend_block(
            state,
            key_block,
            value_block,
            distance,
            grouped_queries,
            doc_start,
            block_index,
            hop_limit,
        )

    carry = absorb(carry, keys, values, 0)
    moving_keys, moving_values = (keys, values)
    for distance in range(1, HOPS + 1):
        moving_keys, moving_values = passed_along((moving_keys, moving_values), SEQ, 1)
        carry = absorb(carry, moving_keys, moving_values, distance)
    top_final, total_final, weighted = carry
    attended = (weighted / total_final[..., None]).reshape(rows, kv_heads * group_size * HEAD_WIDTH)
    attention = attended.astype(jnp.bfloat16)
    marks = loss_mask.astype(jnp.float32)
    local_squares = jnp.sum(marks[:, None] * attended * attended)
    local_count = jnp.sum(marks)
    head_index = lax.axis_index("head")
    share = jnp.where(head_index == 0, local_count, jnp.float32(0.0))
    squares_total, count_total = (over_axes(local_squares, SEQ_HEAD), over_axes(share, SEQ_HEAD))
    objective = squares_total / (QUERY_HEADS * count_total)
    return (attention, objective)


def solution(mesh):
    torus = Mesh(
        mesh.devices.reshape(4, 8, 2, mesh.shape["head"]), ("seq_0", "seq_1", "seq_2", "head")
    )
    placed = (P(SEQ, "head"), P(SEQ, "head"), P(SEQ, "head"), P(SEQ), P(SEQ), P(SEQ))
    return jax.shard_map(
        on_device, mesh=torus, in_specs=placed, out_specs=(P(SEQ, "head"), P()), check_vma=False
    )
```

profile of v0, /device:TPU:1, one launch (start us, length us, event | category | flops | bytes accessed | tf_op | source)
XLA Modules:
  0.0 148.4 jit_solution(18145175230012953295)
XLA Ops:
  0.6 1.1 copy.29
  1.7 4.9 %collective-permute-start = (bf16[512,256]{0,1:T(8,128)(2,1)S(1)}, bf16[512,256]{0,1:T(8,128)(2,1)S(1)}, u32[]{:S(2)}, u32[]{:S(2)}) collective-permute-start(bf16[512,256]{0,1:T(8,128)(2,1)S(1)} %copy.29), channel_id=1, source_target_pairs={{0,4},{4,8},{8,12},{12,16},{16,20},{20,24},{24,28},{28,32},{32,36}... | collective-permute-start | bytes 786440 | tf_op jit(solution)/shard_map/ppermute | solution.py:21
  6.7 1.9 %collective-permute-start.1 = (bf16[512,256]{1,0:T(8,128)(2,1)}, bf16[512,256]{1,0:T(8,128)(2,1)S(1)}, u32[]{:S(2)}, u32[]{:S(2)}) collective-permute-start(bf16[512,256]{1,0:T(8,128)(2,1)} %param.8), channel_id=1, source_target_pairs={{0,4},{4,8},{8,12},{12,16},{16,20},{20,24},{24,28},{28,32},{32,36}... | collective-permute-start | bytes 786440 | tf_op jit(solution)/shard_map/ppermute | solution.py:21
  8.6 1.7 %reshape.416 = bf16[512,2,128]{2,1,0:T(2,128)(2,1)} reshape(bf16[512,256]{1,0:T(8,128)(2,1)} %param.7) | data formatting | bytes 524288 | tf_op jit(solution)/shard_map/reshape | solution.py:68
  10.3 1.1 copy.64
  11.4 0.7 convert_element_type.31
  12.1 1.3 convert_reduce_fusion
  14.2 1.8 %reshape.417 = bf16[512,2,4,128]{3,2,1,0:T(4,128)(2,1)S(1)} reshape(bf16[512,1024]{1,0:T(8,128)(2,1)} %param.6) | data formatting | bytes 2097152 | tf_op jit(solution)/shard_map/reshape | solution.py:60
  16.6 2.1 %and_and_fusion.4 = (pred[512,512]{0,1:T(8,128)(4,1)S(1)}, pred[512,512]{0,1:T(8,128)(4,1)S(1)}, pred[512,512]{0,1:T(8,128)(4,1)S(1)}, pred[512,512]{0,1:T(8,128)(4,1)S(1)}, pred[512,512]{0,1:T(8,128)(4,1)S(1)}) fusion(s32[512]{0:T(512)S(1)} %iota_add_fusion.4, s32[512]{0:T(512)} %param.9, pred[]{:T(512)} %bitcast, pred[]{:T(512)} %bitcast.15, ...), kind=kLoop, calls=%fused_computation.51 | loop fusion | flops 5242880 | bytes 1323013 | tf_op jit(solution)/shard_map/and | solution.py:39
  18.6 5.8 %fusion = (f32[512,2,4]{0,2,1:T(4,128)S(1)}, f32[2,512,512,4]{2,1,3,0:T(8,128)}) fusion(pred[512,512]{0,1:T(8,128)(4,1)S(1)} %get-tuple-element.27, bf16[512,2,4,128]{3,2,1,0:T(4,128)(2,1)S(1)} %reshape.417, bf16[512,2,128,1]{2,1,0,3:T(2,128)(2,1)} %bitcast.160), kind=kOutput, calls=%fused_computation.10 | convolution fusion | flops 543158272 | bytes 9977856 | tf_op jit(solution)/shard_map/tgqd,sgd->tgqs/dot_general | solution.py:33
  24.5 0.0 collective-permute-done.1
  24.5 3.9 %collective-permute-start.3 = (bf16[512,256]{1,0:T(8,128)(2,1)S(1)}, bf16[512,256]{1,0:T(8,128)(2,1)}, u32[]{:S(2)}, u32[]{:S(2)}) collective-permute-start(bf16[512,256]{1,0:T(8,128)(2,1)S(1)} %collective-permute-done.1), channel_id=1, source_target_pairs={{0,4},{4,8},{8,12},{12,16},{16,20},{20,24},{24,28},{28,32},{32,36}... | collective-permute-start | bytes 786440 | tf_op jit(solution)/shard_map/ppermute | solution.py:21
  28.4 0.8 copy.32
  29.2 0.0 collective-permute-done
  29.2 1.9 %collective-permute-start.2 = (bf16[512,256]{0,1:T(8,128)(2,1)S(1)}, bf16[512,256]{0,1:T(8,128)(2,1)S(1)}, u32[]{:S(2)}, u32[]{:S(2)}) collective-permute-start(bf16[512,256]{0,1:T(8,128)(2,1)S(1)} %collective-permute-done), channel_id=1, source_target_pairs={{0,4},{4,8},{8,12},{12,16},{16,20},{20,24},{24,28},{28,32},{32,36}... | collective-permute-start | bytes 786440 | tf_op jit(solution)/shard_map/ppermute | solution.py:21
  31.2 5.0 %fusion.1 = (f32[512,2,4]{0,2,1:T(4,128)S(1)}, f32[2,512,512,4]{2,1,3,0:T(8,128)}) fusion(pred[512,512]{0,1:T(8,128)(4,1)S(1)} %get-tuple-element.31, bf16[512,2,128,1]{0,2,3,1:T(8,128)(2,1)S(1)} %bitcast.155, bf16[512,2,4,128]{3,2,1,0:T(4,128)(2,1)S(1)} %reshape.417), kind=kOutput, calls=%fused_computation.11 | convolution fusion | flops 543158272 | bytes 9977856 | tf_op jit(solution)/shard_map/tgqd,sgd->tgqs/dot_general | solution.py:33
  36.1 0.0 collective-permute-done.3
  36.1 3.9 %collective-permute-start.5 = (bf16[512,256]{1,0:T(8,128)(2,1)}, bf16[512,256]{1,0:T(8,128)(2,1)}, u32[]{:S(2)}, u32[]{:S(2)}) collective-permute-start(bf16[512,256]{1,0:T(8,128)(2,1)} %collective-permute-done.3), channel_id=1, source_target_pairs={{0,4},{4,8},{8,12},{12,16},{16,20},{20,24},{24,28},{28,32},{32,36}... | collective-permute-start | bytes 786440 | tf_op jit(solution)/shard_map/ppermute | solution.py:21
  40.1 1.8 %copy.36 = bf16[512,256]{0,1:T(8,128)(2,1)} copy(bf16[512,256]{1,0:T(8,128)(2,1)} %collective-permute-done.3) | data formatting | bytes 524288 | tf_op jit(solution)/shard_map/ppermute | solution.py:21
  41.9 0.0 collective-permute-done.2
  41.9 1.9 %collective-permute-start.4 = (bf16[512,256]{0,1:T(8,128)(2,1)S(1)}, bf16[512,256]{0,1:T(8,128)(2,1)S(1)}, u32[]{:S(2)}, u32[]{:S(2)}) collective-permute-start(bf16[512,256]{0,1:T(8,128)(2,1)S(1)} %collective-permute-done.2), channel_id=1, source_target_pairs={{0,4},{4,8},{8,12},{12,16},{16,20},{20,24},{24,28},{28,32},{32,36}... | collective-permute-start | bytes 786440 | tf_op jit(solution)/shard_map/ppermute | solution.py:21
  43.8 5.0 %fusion.2 = (f32[512,2,4]{0,2,1:T(4,128)S(1)}, f32[2,512,512,4]{2,1,3,0:T(8,128)}) fusion(pred[512,512]{0,1:T(8,128)(4,1)S(1)} %get-tuple-element.28, bf16[512,2,128,1]{0,2,3,1:T(8,128)(2,1)S(1)} %bitcast.156, bf16[512,2,4,128]{3,2,1,0:T(4,128)(2,1)S(1)} %reshape.417), kind=kOutput, calls=%fused_computation.12 | convolution fusion | flops 543158272 | bytes 9977856 | tf_op jit(solution)/shard_map/tgqd,sgd->tgqs/dot_general | solution.py:33
  48.7 0.0 collective-permute-done.5
  48.7 5.1 %collective-permute-start.7 = (bf16[512,256]{1,0:T(8,128)(2,1)}, bf16[512,256]{1,0:T(8,128)(2,1)}, u32[]{:S(2)}, u32[]{:S(2)}) collective-permute-start(bf16[512,256]{1,0:T(8,128)(2,1)} %collective-permute-done.5), channel_id=1, source_target_pairs={{0,4},{4,8},{8,12},{12,16},{16,20},{20,24},{24,28},{28,32},{32,36}... | collective-permute-start | bytes 786440 | tf_op jit(solution)/shard_map/ppermute | solution.py:21
  53.9 1.8 %copy.40 = bf16[512,256]{0,1:T(8,128)(2,1)} copy(bf16[512,256]{1,0:T(8,128)(2,1)} %collective-permute-done.5) | data formatting | bytes 524288 | tf_op jit(solution)/shard_map/ppermute | solution.py:21
  55.7 0.0 collective-permute-done.4
  55.7 2.1 %collective-permute-start.6 = (bf16[512,256]{0,1:T(8,128)(2,1)S(1)}, bf16[512,256]{0,1:T(8,128)(2,1)S(1)}, u32[]{:S(2)}, u32[]{:S(2)}) collective-permute-start(bf16[512,256]{0,1:T(8,128)(2,1)S(1)} %collective-permute-done.4), channel_id=1, source_target_pairs={{0,4},{4,8},{8,12},{12,16},{16,20},{20,24},{24,28},{28,32},{32,36}... | collective-permute-start | bytes 786440 | tf_op jit(solution)/shard_map/ppermute | solution.py:21
  57.8 0.0 copy-start.3
  57.8 2.2 %fusion.3 = (f32[512,2,4]{0,2,1:T(4,128)S(1)}, f32[2,512,512,4]{2,1,3,0:T(8,128)S(1)}) fusion(pred[512,512]{0,1:T(8,128)(4,1)S(1)} %get-tuple-element.29, bf16[512,2,128,1]{0,2,3,1:T(8,128)(2,1)S(1)} %bitcast.157, bf16[512,2,4,128]{3,2,1,0:T(4,128)(2,1)S(1)} %reshape.417), kind=kOutput, calls=%fused_computation.13 | convolution fusion | flops 543158272 | bytes 9977856 | tf_op jit(solution)/shard_map/tgqd,sgd->tgqs/dot_general | solution.py:33
  60.0 0.9 collective-permute-done.6
  60.9 2.2 %fusion.4 = (f32[512,2,4]{0,2,1:T(4,128)S(1)}, f32[2,512,512,4]{2,1,3,0:T(8,128)S(1)}) fusion(pred[512,512]{0,1:T(8,128)(4,1)S(1)} %get-tuple-element.30, bf16[512,2,128,1]{0,2,3,1:T(8,128)(2,1)S(1)} %bitcast.158, bf16[512,2,4,128]{3,2,1,0:T(4,128)(2,1)S(1)} %reshape.417), kind=kOutput, calls=%fused_computation.14 | convolution fusion | flops 543158272 | bytes 9977856 | tf_op jit(solution)/shard_map/tgqd,sgd->tgqs/dot_general | solution.py:33
  63.1 0.0 copy-start
  63.1 0.0 slice-start.2
  63.1 0.0 copy-done.3
  63.1 0.0 slice-start.3
  63.1 4.0 %fusion.17 = f32[2,512,4,128]{1,3,2,0:T(8,128)} fusion(bf16[512,2,128,1]{0,2,3,1:T(8,128)(2,1)S(1)} %bitcast.163, f32[2,512,512,4]{2,1,3,0:T(8,128)S(1)} %get-tuple-element.35, f32[512,2,4]{0,2,1:T(4,128)S(1)} %get-tuple-element.20, pred[512,512]{0,1:T(8,128)(4,1)S(1)} %get-tuple-element.29), kind=kOutput, calls=%fused_computation.26 | convolution fusion | flops 547356672 | bytes 11026432 | tf_op jit(solution)/shard_map/tgqs,sgd->tgqd/dot_general | solution.py:50
  67.1 1.2 slice-done.2
  68.3 1.9 %slice-done.3 = s8[4194304]{0:T(1024)(128)(4,1)S(1)} async-done(((s8[8388608]{0:T(1024)(128)(4,1)}), s8[4194304]{0:T(1024)(128)(4,1)S(1)}, s32[]{:S(2)}) %slice-start.3) | async-done | bytes 4194328
  70.2 4.0 %fusion.9 = (f32[512,2,4]{0,2,1:T(4,128)S(1)}, f32[512,2,4]{0,2,1:T(4,128)S(1)}) fusion(f32[2,512,512,4]{2,1,3,0:T(8,128)S(1)} %bitcast.151, f32[512,2,4]{0,2,1:T(4,128)S(1)} %get-tuple-element.21, pred[512,512]{0,1:T(8,128)(4,1)S(1)} %get-tuple-element.28, f32[512,2,4]{0,2,1:T(4,128)S(1)} %get-tuple-element.20, ...), kind=kLoop, calls=%fused_computation.19 | loop fusion | flops 20963328 | bytes 17367040 | tf_op jit(solution)/shard_map/reduce_sum | solution.py:48
  74.3 0.0 slice-start
  74.3 0.0 copy-start.1
  74.3 0.0 copy-done.2
  74.3 0.0 slice-start.1
  74.3 4.1 %fusion.19 = f32[2,512,4,128]{1,3,2,0:T(8,128)} fusion(bf16[512,2,128,1]{0,2,3,1:T(8,128)(2,1)S(1)} %bitcast.162, f32[2,512,512,4]{2,1,3,0:T(8,128)S(1)} %bitcast.151, f32[512,2,4]{0,2,1:T(4,128)S(1)} %get-tuple-element.21, pred[512,512]{0,1:T(8,128)(4,1)S(1)} %get-tuple-element.28), kind=kOutput, calls=%fused_computation.27 | convolution fusion | flops 547356672 | bytes 11026432 | tf_op jit(solution)/shard_map/tgqs,sgd->tgqd/dot_general | solution.py:50
  78.4 0.0 slice-done
  78.4 0.0 copy-done.1
  78.4 0.0 slice-done.1
  78.4 0.0 slice-start.5
  78.5 4.0 %fusion.21 = f32[2,512,4,128]{1,3,2,0:T(8,128)} fusion(bf16[512,2,128,1]{0,2,3,1:T(8,128)(2,1)S(1)} %bitcast.161, f32[2,512,512,4]{2,1,3,0:T(8,128)S(1)} %bitcast.149, f32[512,2,4]{0,2,1:T(4,128)S(1)} %get-tuple-element.22, pred[512,512]{0,1:T(8,128)(4,1)S(1)} %get-tuple-element.31), kind=kOutput, calls=%fused_computation.28 | convolution fusion | flops 547356672 | bytes 11026432 | tf_op jit(solution)/shard_map/tgqs,sgd->tgqd/dot_general | solution.py:50
  82.4 0.0 slice-done.4
  82.4 0.0 slice-done.5
  82.4 4.3 %fusion.5 = (f32[512,2,4]{0,2,1:T(4,128)S(1)}, f32[512,2,4]{0,2,1:T(4,128)S(1)}) fusion(f32[2,512,512,4]{2,1,3,0:T(8,128)S(1)} %bitcast.153, f32[512,2,4]{0,2,1:T(4,128)S(1)} %get-tuple-element.26, pred[512,512]{0,1:T(8,128)(4,1)S(1)} %get-tuple-element.27, f32[512,2,4]{0,2,1:T(4,128)S(1)} %get-tuple-element.22, f32[2,512,512,4]{2,1,3,0:T(8,128)S(1)} %bitcast.149, ...), kind=kLoop, calls=%fused_computation.15 | loop fusion | flops 20963328 | bytes 17367040 | tf_op jit(solution)/shard_map/reduce_sum | solution.py:48
  86.7 4.1 %fusion.23 = f32[2,512,4,128]{1,3,2,0:T(8,128)} fusion(bf16[512,2,128,1]{0,2,3,1:T(8,128)(2,1)S(1)} %bitcast.159, f32[2,512,512,4]{2,1,3,0:T(8,128)S(1)} %bitcast.153, f32[512,2,4]{0,2,1:T(4,128)S(1)} %get-tuple-element.26, pred[512,512]{0,1:T(8,128)(4,1)S(1)} %get-tuple-element.27), kind=kOutput, calls=%fused_computation.29 | convolution fusion | flops 547356672 | bytes 11026432 | tf_op jit(solution)/shard_map/tgqs,sgd->tgqd/dot_general | solution.py:50
  90.8 0.0 copy-done
  90.8 2.0 %fusion.13 = f32[512,2,4]{0,2,1:T(4,128)S(1)} fusion(f32[2,512,512,4]{2,1,3,0:T(8,128)S(1)} %get-tuple-element.33, f32[512,2,4]{0,2,1:T(4,128)S(1)} %get-tuple-element.19, pred[512,512]{0,1:T(8,128)(4,1)S(1)} %get-tuple-element.30), kind=kLoop, calls=%fused_computation.23 | loop fusion | flops 10481664 | bytes 8683520 | tf_op jit(solution)/shard_map/reduce_sum | solution.py:48
  92.8 0.1 multiply_add_fusion
  92.9 0.0 collective-permute-done.7
  92.9 1.1 copy.44
  94.0 9.7 %fusion.30 = (f32[]{:T(128)}, bf16[512,2,4,128]{0,3,2,1:T(8,128)(2,1)S(1)}) fusion(f32[512]{0:T(512)S(1)} %convert_element_type.31, f32[512,2,4]{0,2,1:T(4,128)S(1)} %get-tuple-element.14, bf16[512,2,128,1]{0,2,3,1:T(8,128)(2,1)S(1)} %bitcast.164, f32[2,512,512,4]{2,1,3,0:T(8,128)} %copy-done, f32[512,2,4]{0,2,1:T(4,128)S(1)} %get-tuple-element.19, ...), kind=kOutput, calls=%fused_computation.36 | convolution fusion | flops 554696704 | bytes 18466820 | tf_op jit(solution)/shard_map/tgqs,sgd->tgqd/dot_general | solution.py:50
  103.7 1.3 copy.46
  105.0 9.1 %all-reduce.2 = (f32[]{:T(128)}, f32[]{:T(128)}) all-reduce(f32[]{:T(128)} %get-tuple-element.23, f32[]{:T(128)S(6)} %select_n.45), channel_id=1, replica_groups=mesh['seq_0'=4,'seq_1'=8,'seq_2'=2,'head'=4] {'seq_0'}, use_global_device_ids=true, to_apply=%region_11.12 | all-reduce | flops 2 | bytes 16 | tf_op jit(solution)/shard_map/psum | solution.py:25
  114.1 12.1 %all-reduce = (f32[]{:T(128)}, f32[]{:T(128)}) all-reduce(f32[]{:T(128)} %get-tuple-element.10, f32[]{:T(128)} %get-tuple-element.11), channel_id=1, replica_groups=mesh['seq_0'=4,'seq_1'=8,'seq_2'=2,'head'=4] {'seq_1'}, use_global_device_ids=true, to_apply=%region_12.13 | all-reduce | flops 2 | bytes 16 | tf_op jit(solution)/shard_map/psum | solution.py:25
  126.2 10.4 %all-reduce.3 = (f32[]{:T(128)}, f32[]{:T(128)}) all-reduce(f32[]{:T(128)} %get-tuple-element.6, f32[]{:T(128)} %get-tuple-element.7), channel_id=1, replica_groups=mesh['seq_0'=4,'seq_1'=8,'seq_2'=2,'head'=4] {'seq_2'}, use_global_device_ids=true, to_apply=%region_13.14 | all-reduce | flops 2 | bytes 16 | tf_op jit(solution)/shard_map/psum | solution.py:25
  136.6 9.4 %all-reduce.1 = (f32[]{:T(128)}, f32[]{:T(128)}) all-reduce(f32[]{:T(128)} %get-tuple-element.12, f32[]{:T(128)} %get-tuple-element.13), channel_id=1, replica_groups=mesh['seq_0'=4,'seq_1'=8,'seq_2'=2,'head'=4] {'head'}, use_global_device_ids=true, to_apply=%region_14.15 | all-reduce | flops 2 | bytes 16 | tf_op jit(solution)/shard_map/psum | solution.py:25
  (11 shorter events, 0.1 us)
Async XLA Ops:
  1.7 27.5 %collective-permute-start = (bf16[512,256]{0,1:T(8,128)(2,1)S(1)}, bf16[512,256]{0,1:T(8,128)(2,1)S(1)}, u32[]{:S(2)}, u32[]{:S(2)}) collective-permute-start(bf16[512,256]{0,1:T(8,128)(2,1)S(1)} %copy.29), channel_id=1, source_target_pairs={{0,4},{4,8},{8,12},{12,16},{16,20},{20,24},{24,28},{28,32},{32,36}... | collective-permute-start | bytes 786440 | tf_op jit(solution)/shard_map/ppermute | solution.py:21
  6.7 17.8 %collective-permute-start.1 = (bf16[512,256]{1,0:T(8,128)(2,1)}, bf16[512,256]{1,0:T(8,128)(2,1)S(1)}, u32[]{:S(2)}, u32[]{:S(2)}) collective-permute-start(bf16[512,256]{1,0:T(8,128)(2,1)} %param.8), channel_id=1, source_target_pairs={{0,4},{4,8},{8,12},{12,16},{16,20},{20,24},{24,28},{28,32},{32,36}... | collective-permute-start | bytes 786440 | tf_op jit(solution)/shard_map/ppermute | solution.py:21
  24.5 11.6 %collective-permute-start.3 = (bf16[512,256]{1,0:T(8,128)(2,1)S(1)}, bf16[512,256]{1,0:T(8,128)(2,1)}, u32[]{:S(2)}, u32[]{:S(2)}) collective-permute-start(bf16[512,256]{1,0:T(8,128)(2,1)S(1)} %collective-permute-done.1), channel_id=1, source_target_pairs={{0,4},{4,8},{8,12},{12,16},{16,20},{20,24},{24,28},{28,32},{32,36}... | collective-permute-start | bytes 786440 | tf_op jit(solution)/shard_map/ppermute | solution.py:21
  29.2 12.6 %collective-permute-start.2 = (bf16[512,256]{0,1:T(8,128)(2,1)S(1)}, bf16[512,256]{0,1:T(8,128)(2,1)S(1)}, u32[]{:S(2)}, u32[]{:S(2)}) collective-permute-start(bf16[512,256]{0,1:T(8,128)(2,1)S(1)} %collective-permute-done), channel_id=1, source_target_pairs={{0,4},{4,8},{8,12},{12,16},{16,20},{20,24},{24,28},{28,32},{32,36}... | collective-permute-start | bytes 786440 | tf_op jit(solution)/shard_map/ppermute | solution.py:21
  36.1 12.6 %collective-permute-start.5 = (bf16[512,256]{1,0:T(8,128)(2,1)}, bf16[512,256]{1,0:T(8,128)(2,1)}, u32[]{:S(2)}, u32[]{:S(2)}) collective-permute-start(bf16[512,256]{1,0:T(8,128)(2,1)} %collective-permute-done.3), channel_id=1, source_target_pairs={{0,4},{4,8},{8,12},{12,16},{16,20},{20,24},{24,28},{28,32},{32,36}... | collective-permute-start | bytes 786440 | tf_op jit(solution)/shard_map/ppermute | solution.py:21
  41.9 13.8 %collective-permute-start.4 = (bf16[512,256]{0,1:T(8,128)(2,1)S(1)}, bf16[512,256]{0,1:T(8,128)(2,1)S(1)}, u32[]{:S(2)}, u32[]{:S(2)}) collective-permute-start(bf16[512,256]{0,1:T(8,128)(2,1)S(1)} %collective-permute-done.2), channel_id=1, source_target_pairs={{0,4},{4,8},{8,12},{12,16},{16,20},{20,24},{24,28},{28,32},{32,36}... | collective-permute-start | bytes 786440 | tf_op jit(solution)/shard_map/ppermute | solution.py:21
  48.7 44.2 %collective-permute-start.7 = (bf16[512,256]{1,0:T(8,128)(2,1)}, bf16[512,256]{1,0:T(8,128)(2,1)}, u32[]{:S(2)}, u32[]{:S(2)}) collective-permute-start(bf16[512,256]{1,0:T(8,128)(2,1)} %collective-permute-done.5), channel_id=1, source_target_pairs={{0,4},{4,8},{8,12},{12,16},{16,20},{20,24},{24,28},{28,32},{32,36}... | collective-permute-start | bytes 786440 | tf_op jit(solution)/shard_map/ppermute | solution.py:21
  55.7 5.2 %collective-permute-start.6 = (bf16[512,256]{0,1:T(8,128)(2,1)S(1)}, bf16[512,256]{0,1:T(8,128)(2,1)S(1)}, u32[]{:S(2)}, u32[]{:S(2)}) collective-permute-start(bf16[512,256]{0,1:T(8,128)(2,1)S(1)} %collective-permute-done.4), channel_id=1, source_target_pairs={{0,4},{4,8},{8,12},{12,16},{16,20},{20,24},{24,28},{28,32},{32,36}... | collective-permute-start | bytes 786440 | tf_op jit(solution)/shard_map/ppermute | solution.py:21
  57.8 5.3 %copy-start.3 = (bf16[512,256]{0,1:T(8,128)(2,1)S(1)}, bf16[512,256]{0,1:T(8,128)(2,1)}, u32[]{:S(2)}) copy-start(bf16[512,256]{0,1:T(8,128)(2,1)} %copy.40) | copy-start | bytes 786436
  63.1 27.7 %copy-start = (f32[2,512,512,4]{2,1,3,0:T(8,128)}, f32[2,512,512,4]{2,1,3,0:T(8,128)S(1)}, u32[]{:S(2)}) copy-start(f32[2,512,512,4]{2,1,3,0:T(8,128)S(1)} %get-tuple-element.33) | copy-start | bytes 25165828
  63.1 5.3 %slice-start.2 = ((s8[8388608]{0:T(1024)(128)(4,1)}), s8[4194304]{0:T(1024)(128)(4,1)S(1)}, s32[]{:S(2)}) async-start(s8[8388608]{0:T(1024)(128)(4,1)} %bitcast.150), calls=%async_computation.2 | async-start | bytes 8388608
  63.1 7.1 %slice-start.3 = ((s8[8388608]{0:T(1024)(128)(4,1)}), s8[4194304]{0:T(1024)(128)(4,1)S(1)}, s32[]{:S(2)}) async-start(s8[8388608]{0:T(1024)(128)(4,1)} %bitcast.150), calls=%async_computation.3 | async-start | bytes 8388608
  70.2 4.1 %copy-start.2 = (bf16[512,256]{0,1:T(8,128)(2,1)S(1)}, bf16[512,256]{0,1:T(8,128)(2,1)}, u32[]{:S(2)}) copy-start(bf16[512,256]{0,1:T(8,128)(2,1)} %copy.36) | copy-start | bytes 786436
  74.3 4.1 %slice-start = ((s8[8388608]{0:T(1024)(128)(4,1)}), s8[4194304]{0:T(1024)(128)(4,1)S(1)}, s32[]{:S(2)}) async-start(s8[8388608]{0:T(1024)(128)(4,1)} %bitcast.148), calls=%async_computation | async-start | bytes 8388608
  74.3 4.1 %copy-start.1 = (bf16[512,256]{0,1:T(8,128)(2,1)S(1)}, bf16[512,256]{0,1:T(8,128)(2,1)}, u32[]{:S(2)}) copy-start(bf16[512,256]{0,1:T(8,128)(2,1)} %copy.32) | copy-start | bytes 786436
  74.3 4.1 %slice-start.1 = ((s8[8388608]{0:T(1024)(128)(4,1)}), s8[4194304]{0:T(1024)(128)(4,1)S(1)}, s32[]{:S(2)}) async-start(s8[8388608]{0:T(1024)(128)(4,1)} %bitcast.148), calls=%async_computation.1 | async-start | bytes 8388608
  78.4 4.0 %slice-start.4 = ((s8[8388608]{0:T(1024)(128)(4,1)}), s8[4194304]{0:T(1024)(128)(4,1)S(1)}, s32[]{:S(2)}) async-start(s8[8388608]{0:T(1024)(128)(4,1)} %bitcast.152), calls=%async_computation.4 | async-start | bytes 8388608
  78.4 4.0 %slice-start.5 = ((s8[8388608]{0:T(1024)(128)(4,1)}), s8[4194304]{0:T(1024)(128)(4,1)S(1)}, s32[]{:S(2)}) async-start(s8[8388608]{0:T(1024)(128)(4,1)} %bitcast.152), calls=%async_computation.5 | async-start | bytes 8388608
where the time goes:
time: 149 us; the launch traced here: 148 us
  matrix products  45.9 us (31%)
  blocking collectives  41 us (28%)
  starting transfers between devices  25.7 us (17%)
  local copies, waits for them, and re-layouts  15.7 us (11%)
  other arithmetic  14.5 us (10%)
  between operations  4.69 us (3%)
    psum x4, blocking collectives, over_axes(): return functools.reduce(lax.psum, axes, shard)  41 us
    dot_general x5, matrix products, attend_block(): jnp.einsum('tgqs,sgd->tgqd', rounded, value_block, preferred_element_type...  25.8 us
    ppermute x8, starting transfers between devices, passed_along(): return lax.ppermute(shard, axis, pairs)  25.7 us
    dot_general x5, matrix products, attend_block(): jnp.einsum('tgqd,sgd->tgqs', grouped_queries, key_block, preferred_elemen...  20.1 us
    reduce_sum x3, other arithmetic, attend_block(): total_new = total_old * ratio_old + jnp.sum(weights, axis=-1)  10.4 us
    ppermute x4, local copies, waits for them, and re-layouts, passed_along(): return lax.ppermute(shard, axis, pairs)  5.55 us
    unnamed x22, local copies, waits for them, and re-layouts  5.54 us
  transfers between devices with their start and end apart: 8, of which 1 were waited for; matrix products, arithmetic and copies ran while one was open for 40% of the time, Pallas kernels for 0%

commit v1 on v0

v1 whole, which is shorter than its diff:
```python
import functools
import math

import jax
import jax.numpy as jnp
from jax import lax
from jax.experimental import pallas as pl
from jax.experimental.pallas import tpu as pltpu
from jax.sharding import Mesh
from jax.sharding import PartitionSpec as P

QUERY_HEADS = 32
KEY_VALUE_HEADS = 8
HEAD_WIDTH = 128
HOPS = 4
GROUP = QUERY_HEADS // KEY_VALUE_HEADS
CHUNKS = 4
SEQ = ("seq_0", "seq_1", "seq_2")
MESH = pl.DeviceIdType.MESH
EXP_SCALE = math.log2(math.e) / math.sqrt(HEAD_WIDTH)
HIDDEN = -1e30


def kernel(
    sizes,
    q_hbm,
    k_hbm,
    v_hbm,
    doc_ref,
    hop_ref,
    mark_ref,
    out_hbm,
    obj_ref,
    kv,
    q_in,
    q_t,
    acc,
    top,
    total,
    bias,
    out_vm,
    parts_c,
    parts_h,
    parts_x,
    parts_z,
    load_sem,
    store_sem,
    send_sem,
    recv_sem,
    part_send,
    part_recv,
):
    nx, nz, nc, nh = sizes
    rows = q_in.shape[0]
    kv_heads = kv.shape[3] // HEAD_WIDTH
    heads = kv_heads * GROUP
    step_rows = rows // CHUNKS
    ix, iz, ic, ih = (lax.axis_index(a) for a in (*SEQ, "head"))
    chip = ix * nz + iz
    block = chip * nc + ic
    after = lax.rem(chip + 1, nx * nz)
    before = lax.rem(chip + nx * nz - 1, nx * nz)
    next_chip = {"seq_0": after // nz, "seq_1": lax.rem(after, nz)}
    last_chip = {"seq_0": before // nz, "seq_1": lax.rem(before, nz)}
    partner = {"seq_2": 1 - ic}
    axes = (("seq_2", nc, ic), ("head", nh, ih), ("seq_0", nx, ix), ("seq_1", nz, iz))

    loads = (
        pltpu.make_async_copy(k_hbm, kv.at[0, 0], load_sem.at[0]),
        pltpu.make_async_copy(v_hbm, kv.at[0, 1], load_sem.at[1]),
        pltpu.make_async_copy(q_hbm, q_in, load_sem.at[2]),
    )
    for load in loads:
        load.start()

    barrier = pltpu.get_barrier_semaphore()
    signals = 2
    pl.semaphore_signal(barrier, inc=1, device_id=next_chip, device_id_type=MESH)
    pl.semaphore_signal(barrier, inc=1, device_id=last_chip, device_id_type=MESH)
    for name, size, here in axes:
        for d in range(1, size):
            pl.semaphore_signal(
                barrier, inc=1, device_id={name: lax.rem(here + d, size)}, device_id_type=MESH
            )
            signals += 1
    loads[0].wait()
    loads[1].wait()
    pl.semaphore_wait(barrier, signals)

    def piece(slot, c):
        return kv.at[slot, :, pl.ds(pl.multiple_of(c * step_rows, step_rows), step_rows), :]

    def hand_on(kind, slot, c, to_slot, device):
        return pltpu.make_async_remote_copy(
            src_ref=piece(slot, c),
            dst_ref=piece(to_slot, c),
            send_sem=send_sem.at[kind, c],
            recv_sem=recv_sem.at[to_slot, c],
            device_id=device,
            device_id_type=MESH,
        )

    def arrived(slot, c):
        hand_on(0, 0, c, slot, next_chip).wait_recv()

    for c in range(CHUNKS):
        hand_on(0, 0, c, 2, next_chip).start()

    @pl.when(ic == 0)
    def _():
        for c in range(CHUNKS):
            hand_on(2, 0, c, 1, partner).start()

    loads[2].wait()
    for h in range(heads):
        q_t[h] = q_in[:, h * HEAD_WIDTH : (h + 1) * HEAD_WIDTH].T
    top[...] = jnp.full(top.shape, HIDDEN, jnp.float32)
    total[...] = jnp.zeros(total.shape, jnp.float32)
    acc[...] = jnp.zeros(acc.shape, jnp.float32)

    first_key = jnp.maximum(doc_ref[...], (block - hop_ref[0]) * rows)
    q_place = block * rows + lax.broadcasted_iota(jnp.int32, (1, rows), 1)

    def attend(slot_a, c_a, slot_b, c_b):
        at_a = pl.ds(pl.multiple_of(c_a * step_rows, step_rows), step_rows)
        at_b = pl.ds(pl.multiple_of(c_b * step_rows, step_rows), step_rows)
        inside = lax.broadcasted_iota(jnp.int32, (step_rows, rows), 0)
        for i, (slot, c) in enumerate(((slot_a, c_a), (slot_b, c_b))):
            place = inside + ((block - slot) * rows + c * step_rows)
            seen = (place >= first_key) & (place <= q_place)
            bias[i * step_rows : (i + 1) * step_rows, :] = jnp.where(seen, 0.0, HIDDEN)
        for g in range(kv_heads):
            lanes = slice(g * HEAD_WIDTH, (g + 1) * HEAD_WIDTH)
            k_two = jnp.concatenate([kv[slot_a, 0, at_a, lanes], kv[slot_b, 0, at_b, lanes]], 0)
            v_two = jnp.concatenate([kv[slot_a, 1, at_a, lanes], kv[slot_b, 1, at_b, lanes]], 0)
            v_t = v_two.T
            for h in range(g * GROUP, (g + 1) * GROUP):
                scores = jnp.dot(k_two, q_t[h], preferred_element_type=jnp.float32) + bias[...]
                old = top[h : h + 1, :]
                new = jnp.maximum(old, jnp.max(scores, axis=0, keepdims=True))
                weights = jnp.exp2((scores - new) * EXP_SCALE)
                ratio = jnp.exp2((old - new) * EXP_SCALE)
                total[h : h + 1, :] = total[h : h + 1, :] * ratio + jnp.sum(
                    weights, axis=0, keepdims=True
                )
                update = jnp.dot(
                    v_t, weights.astype(jnp.bfloat16), preferred_element_type=jnp.float32
                )
                acc[h] = acc[h] * ratio + update
                top[h : h + 1, :] = new

    def own(i, _):
        attend(0, 2 * i, 0, 2 * i + 1)
        return 0

    lax.fori_loop(0, CHUNKS // 2, own, 0)

    def neighbour(i, _):
        arrived(1, 2 * i)
        arrived(1, 2 * i + 1)
        attend(1, 2 * i, 1, 2 * i + 1)
        return 0

    lax.fori_loop(0, jnp.where(ic == 1, CHUNKS // 2, 0), neighbour, 0)

    mixed = jnp.where(ic == 0, 1, 3)

    def middle(c, _):
        arrived(2, c)
        hand_on(1, 2, c, 4, next_chip).start()
        hand_on(3, 2, c, 4 - mixed, partner).start()
        arrived(mixed, c)
        attend(2, c, mixed, c)
        return 0

    lax.fori_loop(0, CHUNKS, middle, 0)

    @pl.when(ic == 0)
    def _():
        def far(c, _):
            arrived(4, c)
            arrived(3, c)
            attend(4, c, 3, c)
            return 0

        lax.fori_loop(0, CHUNKS, far, 0)

    @pl.when(ic == 1)
    def _():
        def far(i, _):
            for c in (2 * i, 2 * i + 1):
                arrived(4, c)
                hand_on(4, 4, c, 3, partner).start()
            attend(4, 2 * i, 4, 2 * i + 1)
            return 0

        lax.fori_loop(0, CHUNKS // 2, far, 0)

    marks = mark_ref[...].astype(jnp.float32)
    squares = jnp.zeros((1, rows), jnp.float32)
    for h in range(heads):
        attended = acc[h] * (1.0 / total[h : h + 1, :])
        squares = squares + jnp.sum(attended * attended, axis=0, keepdims=True)
        out_vm[:, h * HEAD_WIDTH : (h + 1) * HEAD_WIDTH] = attended.astype(jnp.bfloat16).T
    store = pltpu.make_async_copy(out_vm, out_hbm, store_sem)
    store.start()

    def folded(row):
        return sum(row[:, i : i + 128] for i in range(0, rows, 128))

    part = jnp.concatenate([folded(marks * squares), folded(marks)], 0)
    sent = []
    for stage, ((name, size, here), parts) in enumerate(
        zip(axes, (parts_c, parts_h, parts_x, parts_z), strict=True)
    ):
        parts[here] = part
        copies = []
        for d in range(1, size):
            peer = lax.rem(here + d, size)
            copy = pltpu.make_async_remote_copy(
                src_ref=parts.at[here],
                dst_ref=parts.at[here],
                send_sem=part_send.at[stage, d],
                recv_sem=part_recv.at[stage, here],
                device_id={name: peer},
                device_id_type=MESH,
            )
            copy.start()
            copies.append(copy)
        for d in range(1, size):
            peer = lax.rem(here + d, size)
            pltpu.make_async_remote_copy(
                src_ref=parts.at[here],
                dst_ref=parts.at[peer],
                send_sem=part_send.at[stage, d],
                recv_sem=part_recv.at[stage, peer],
                device_id={name: peer},
                device_id_type=MESH,
            ).wait_recv()
        part = parts[0]
        for i in range(1, size):
            part = part + parts[i]
        sent += copies
    objective = jnp.sum(part[0:1, :]) / ((QUERY_HEADS // nh) * jnp.sum(part[1:2, :]))
    obj_ref[0, 0] = objective

    for copy in sent:
        copy.wait_send()
    for c in range(CHUNKS):
        hand_on(0, 0, c, 2, next_chip).wait_send()
        hand_on(1, 2, c, 4, next_chip).wait_send()
        hand_on(3, 2, c, 4 - mixed, partner).wait_send()

    @pl.when(ic == 0)
    def _():
        for c in range(CHUNKS):
            hand_on(2, 0, c, 1, partner).wait_send()

    @pl.when(ic == 1)
    def _():
        for c in range(CHUNKS):
            hand_on(4, 4, c, 3, partner).wait_send()

    store.wait()


def on_device(sizes, queries, keys, values, doc_start, hop_counts, loss_mask):
    nx, nz, nc, nh = sizes
    rows, width = queries.shape
    kv_width = keys.shape[1]
    heads = width // HEAD_WIDTH
    most = max(sizes)
    attention, objective = pl.pallas_call(
        functools.partial(kernel, sizes),
        out_shape=(
            jax.ShapeDtypeStruct((rows, width), jnp.bfloat16),
            jax.ShapeDtypeStruct((1, 1), jnp.float32),
        ),
        in_specs=[
            pl.BlockSpec(memory_space=pl.ANY),
            pl.BlockSpec(memory_space=pl.ANY),
            pl.BlockSpec(memory_space=pl.ANY),
            pl.BlockSpec(memory_space=pltpu.VMEM),
            pl.BlockSpec(memory_space=pltpu.SMEM),
            pl.BlockSpec(memory_space=pltpu.VMEM),
        ],
        out_specs=(
            pl.BlockSpec(memory_space=pl.ANY),
            pl.BlockSpec(memory_space=pltpu.SMEM),
        ),
        scratch_shapes=[
            pltpu.VMEM((HOPS + 1, 2, rows, kv_width), jnp.bfloat16),
            pltpu.VMEM((rows, width), jnp.bfloat16),
            pltpu.VMEM((heads, HEAD_WIDTH, rows), jnp.bfloat16),
            pltpu.VMEM((heads, HEAD_WIDTH, rows), jnp.float32),
            pltpu.VMEM((heads, rows), jnp.float32),
            pltpu.VMEM((heads, rows), jnp.float32),
            pltpu.VMEM((2 * rows // CHUNKS, rows), jnp.float32),
            pltpu.VMEM((rows, width), jnp.bfloat16),
            pltpu.VMEM((nc, 2, 128), jnp.float32),
            pltpu.VMEM((nh, 2, 128), jnp.float32),
            pltpu.VMEM((nx, 2, 128), jnp.float32),
            pltpu.VMEM((nz, 2, 128), jnp.float32),
            pltpu.SemaphoreType.DMA((3,)),
            pltpu.SemaphoreType.DMA,
            pltpu.SemaphoreType.DMA((5, CHUNKS)),
            pltpu.SemaphoreType.DMA((HOPS + 1, CHUNKS)),
            pltpu.SemaphoreType.DMA((4, most)),
            pltpu.SemaphoreType.DMA((4, most)),
        ],
        compiler_params=pltpu.CompilerParams(collective_id=0, has_side_effects=True),
    )(
        queries,
        keys,
        values,
        doc_start.reshape(1, rows),
        hop_counts,
        loss_mask.reshape(1, rows),
    )
    return attention, objective.reshape(())


def solution(mesh):
    nh = mesh.shape["head"]
    devices = mesh.devices.reshape(4, 8, 2, nh)
    torus = Mesh(devices, (*SEQ, "head"))
    placed = (P(SEQ, "head"), P(SEQ, "head"), P(SEQ, "head"), P(SEQ), P(SEQ), P(SEQ))
    return jax.shard_map(
        functools.partial(on_device, devices.shape),
        mesh=torus,
        in_specs=placed,
        out_specs=(P(SEQ, "head"), P()),
        check_vma=False,
    )
```

time: 149 us -> 68.4 us (0.46)
  Pallas kernels: 0 us -> 63 us
  matrix products: 45.9 us -> 0 us
  blocking collectives: 41 us -> 0 us
  starting transfers between devices: 25.7 us -> 0 us
  other arithmetic: 14.5 us -> 0 us
  local copies, waits for them, and re-layouts: 15.7 us -> 2.26 us
  between operations: 4.69 us -> 2.97 us
    pallas_call x0 -> x1, Pallas kernels: none -> 63 us  [on_device(): pl.pallas_call(functools.partial(kernel, sizes), out_shape=(jax.ShapeDtyp...]
    dot_general x10 -> x0, matrix products: 45.9 us -> none  [the longest x5 25.8 us: attend_block(): jnp.einsum('tgqs,sgd->tgqd', rounded, value_block, preferred_element_type...]
    psum x4 -> x0, blocking collectives: 41 us -> none  [over_axes(): return functools.reduce(lax.psum, axes, shard)]
    ppermute x8 -> x0, starting transfers between devices: 25.7 us -> none  [passed_along(): return lax.ppermute(shard, axis, pairs)]
    reduce_sum x4 -> x0, other arithmetic: 11.7 us -> none  [the longest x3 10.4 us: attend_block(): total_new = total_old * ratio_old + jnp.sum(weights, axis=-1)]
    ppermute x4 -> x0, local copies, waits for them, and re-layouts: 5.55 us -> none  [passed_along(): return lax.ppermute(shard, axis, pairs)]
    reshape x3 -> x0, local copies, waits for them, and re-layouts: 4.6 us -> none  [the longest x1 1.79 us: on_device(): grouped_queries = queries.reshape(rows, kv_heads, group_size, HEAD_WIDTH)]
    unnamed x22 -> x1, local copies, waits for them, and re-layouts: 5.54 us -> 2.26 us
  transfers between devices with their start and end apart: 8 -> 0, of which waited for: 1 -> 0; matrix products, arithmetic and copies ran while one was open for 40% -> 0% of each run, Pallas kernels for 0% -> 0%
where the time goes in v1:
time: 68.4 us; the launch traced here: 68.3 us
  Pallas kernels  63 us (92%)
  between operations  2.97 us (4%)
  local copies, waits for them, and re-layouts  2.26 us (3%)
    pallas_call x1, Pallas kernels, on_device(): pl.pallas_call(functools.partial(kernel, sizes), out_shape=(jax.ShapeDtyp...  63 us
    unnamed x1, local copies, waits for them, and re-layouts  2.26 us

profile of v1, /device:TPU:1, one launch (start us, length us, event | category | flops | bytes accessed | tf_op | source)
XLA Modules:
  0.0 68.3 jit_solution(8401452056326112041)
XLA Ops:
  1.3 63.0 %shard_map.77 = (bf16[512,1024]{1,0:T(8,128)(2,1)}, f32[1,1]{1,0:T(1,128)}) custom-call(bf16[512,1024]{1,0:T(8,128)(2,1)} %q_hbm.1, bf16[512,256]{1,0:T(8,128)(2,1)} %k_hbm.1, bf16[512,256]{1,0:T(8,128)(2,1)} %v_hbm.1, s32[1,512]{1,0:T(1,128)} %bitcast.3, s32[1]{0:T(128)S(6)} %copy.10.hop_ref, s32[1,512]{1,0:T(1,128)} %bitcast.4), custom_call_target="tpu_custom_call" | custom-call | tf_op jit(solution)/shard_map/pallas_call | solution.py:273
  64.3 2.3 %copy.11 = bf16[512,1024]{1,0:T(8,128)(2,1)} copy(bf16[512,1024]{1,0:T(8,128)(2,1)} %get-tuple-element.8) | data formatting | bytes 2097152
